TPU v7x, 32 devices: a whole 2x2x4 slice. The times are simulated.
32 devices in a mesh: groups: 2 (over y), tok: 8 (over z, core), head: 2 (over x), pair: 1.
Axes of the slice: x: 2, y: 2, z: 4, core: 2. Of those that a mesh axis runs over, the one named last changes fastest.
Arguments:
- queries: bfloat16 [2048, 4096], P(('groups', 'tok'), ('head', 'pair')), parts along dimension 0, may hold values from -6 to 6
- keys_values: bfloat16 [2048, 1024], P(('groups', 'tok'), ('head', 'pair')), parts along dimension 0, may hold values from -6 to 6
- sink_logits: float32 [64], P(('head', 'pair')), may hold values from -2 to 3
- residual: bfloat16 [2048, 2880], P(('groups', 'tok')), parts along dimension 0, may hold values from -60 to 60
- out_weight: bfloat16 [4096, 2880], P(('head', 'pair')), may hold values from -0.09375 to 0.09375
- norm_gain: float32 [2880], replicated, may hold values from 0.5 to 1.5
- expert_ids: int32 [2048, 4], P(('groups', 'tok')), parts along dimension 0, may hold values from 0 to 7, all different within a row; in each aligned block of 128 rows (0 to 127, 128 to 255, ...) at most 80 rows name the same one
- route_weights: float32 [2048, 4], P(('groups', 'tok')), parts along dimension 0, may hold values from 0.1 to 1
- gate_up: bfloat16 [8, 2880, 2, 1440], P('tok', None, None, ('head', 'pair')), may hold values from -0.109375 to 0.109375
- down_weight: bfloat16 [8, 1440, 2880], P('tok', ('head', 'pair')), may hold values from -0.21875 to 0.21875
Outputs:
- layer_output: bfloat16 [2048, 2880], P(('groups', 'tok'), ('head', 'pair')), parts along dimension 0
There are 2 independent parts, one for each index of `groups`. A program takes and returns all parts, laid end to end along the dimension named above; an argument that names none is the same for every part. Nothing has to cross between parts.
Inputs may be any that keep to these rules, and one draw needn't show every extreme that they name: `expert_ids`: in each aligned block of 128 rows (the rows of one index of tok), a row names 4 different experts and no expert is named by more than 80 rows.
All inputs are finite; a program needn't handle non-finite values.
Results may differ from a plain program's by a relative error of at most 0.01.
Values may be sent and summed in bfloat16 or wider, within the bound.
A program may use at most 128 MiB of HBM per device.

v0:
```python
import jax
import jax.numpy as jnp
from jax import lax
from jax.sharding import PartitionSpec as P

HEAD_DIM = 64


def slot_places(expert_ids, experts, capacity):
    tok_rows = expert_ids.shape[0]
    fanout = expert_ids.shape[1]
    flat_ids = expert_ids.reshape(-1)
    one_hot = (flat_ids[:, None] == jnp.arange(experts, dtype=jnp.int32)[None, :]).astype(jnp.int32)
    earlier = jnp.cumsum(one_hot, axis=0) - one_hot
    ranking = jnp.sum(earlier * one_hot, axis=1)
    targets = flat_ids * capacity + ranking
    sources = jnp.arange(tok_rows * fanout, dtype=jnp.int32) // fanout
    table = jnp.full((experts * capacity,), tok_rows, jnp.int32).at[targets].set(sources)
    return (targets.reshape(tok_rows, fanout), table)


def active_rows(flat_rows, gate_up):
    local_hidden = gate_up.shape[-1]
    both_columns = gate_up.reshape(flat_rows.shape[-1], 2 * local_hidden)
    both = jnp.dot(flat_rows, both_columns, preferred_element_type=jnp.float32)
    gate_part = both[:, :local_hidden]
    up_part = both[:, local_hidden:]
    return (gate_part * jax.nn.sigmoid(1.702 * gate_part) * (up_part + 1.0)).astype(jnp.bfloat16)


def per_device(
    queries,
    keys_values,
    sink_logits,
    residual,
    out_weight,
    norm_gain,
    expert_ids,
    route_weights,
    gate_up,
    down_weight,
):
    tok_rows = queries.shape[0]
    kv_groups = keys_values.shape[1] // (2 * HEAD_DIM)
    local_heads = queries.shape[1] // HEAD_DIM
    repeat = local_heads // kv_groups
    position = lax.axis_index("tok") * tok_rows + jnp.arange(tok_rows, dtype=jnp.int32)
    grouped = queries.reshape(tok_rows, kv_groups, repeat, HEAD_DIM)
    start_max = jnp.broadcast_to(
        sink_logits.reshape(kv_groups, repeat)[:, :, None], (kv_groups, repeat, tok_rows)
    )
    start_totals = jnp.ones((kv_groups, repeat, tok_rows), jnp.float32)
    start_accum = jnp.zeros((kv_groups, repeat, tok_rows, HEAD_DIM), jnp.float32)
    key_piece = lax.all_gather(keys_values, "tok", axis=0, tiled=True)
    totals = start_totals
    accum = start_accum
    count = key_piece.shape[0]
    split_piece = key_piece.reshape(count, kv_groups, 2, HEAD_DIM)
    scores = (
        jnp.einsum(
            "tgrd,ngd->grtn", grouped, split_piece[:, :, 0], preferred_element_type=jnp.float32
        )
        * 0.125
    )
    key_position = jnp.arange(count, dtype=jnp.int32)
    allowed = key_position[None, :] <= position[:, None]
    scores = jnp.where(allowed, scores, jnp.float32(-1e30))
    new_max = jnp.maximum(start_max, jnp.max(scores, axis=-1))
    decay = jnp.exp(start_max - new_max)
    weights = jnp.exp(scores - new_max[..., None])
    totals = totals * decay + jnp.sum(weights, axis=-1)
    update = jnp.einsum(
        "grtn,ngd->grtd",
        weights.astype(jnp.bfloat16),
        split_piece[:, :, 1],
        preferred_element_type=jnp.float32,
    )
    accum = accum * decay[..., None] + update
    final_max, totals, accum = (new_max, totals, accum)
    attended = (accum / totals[..., None]).astype(jnp.bfloat16)
    attended = jnp.transpose(attended, (2, 0, 1, 3)).reshape(tok_rows, local_heads * HEAD_DIM)
    width = out_weight.shape[1]
    experts = lax.axis_size("tok")
    fanout = expert_ids.shape[1]
    capacity = min(tok_rows, tok_rows * fanout * 5 // (4 * experts))
    targets, table = slot_places(expert_ids, experts, capacity)
    share = width // lax.axis_size(("head", "pair"))
    column_start = lax.axis_index(("head", "pair")) * share
    partial_value = jnp.dot(attended, out_weight, preferred_element_type=jnp.float32)
    projected = lax.psum(partial_value.astype(jnp.bfloat16), ("head", "pair")).astype(jnp.float32)
    stream = residual.astype(jnp.float32) + projected
    inverse = lax.rsqrt(jnp.mean(stream * stream, axis=-1, keepdims=True) + 1e-05)
    normed = (stream * inverse * norm_gain).astype(jnp.bfloat16)
    padded = jnp.concatenate([normed, jnp.zeros((1, width), jnp.bfloat16)], axis=0)
    outgoing = padded[table].reshape(experts, capacity, width)
    received = lax.all_to_all(outgoing, "tok", split_axis=0, concat_axis=0, tiled=True)
    shape_in = received.shape
    active = active_rows(received.reshape(-1, shape_in[-1]), gate_up)
    partial_value = jnp.dot(active, down_weight[0], preferred_element_type=jnp.float32)
    partial_out = partial_value.reshape(shape_in[:-1] + (partial_value.shape[-1],))
    stream_share = lax.dynamic_slice_in_dim(stream, column_start, share, 1)
    expert_out = lax.psum_scatter(
        partial_out.astype(jnp.bfloat16), ("head", "pair"), scatter_dimension=2, tiled=True
    )
    returned = lax.all_to_all(expert_out, "tok", split_axis=0, concat_axis=0, tiled=True)
    flat_out = returned.reshape(experts * capacity, share)
    picked = flat_out[targets]
    mixture = jnp.sum(route_weights[:, :, None] * picked.astype(jnp.float32), axis=1)
    return (stream_share + mixture).astype(jnp.bfloat16)


def solution(mesh):
    placed = (
        P(("groups", "tok"), ("head", "pair")),
        P(("groups", "tok"), ("head", "pair")),
        P(("head", "pair")),
        P(("groups", "tok"), None),
        P(("head", "pair"), None),
        P(),
        P(("groups", "tok"), None),
        P(("groups", "tok"), None),
        P("tok", None, None, ("head", "pair")),
        P("tok", ("head", "pair"), None),
    )
    return jax.shard_map(
        per_device,
        mesh=mesh,
        in_specs=placed,
        out_specs=P(("groups", "tok"), ("head", "pair")),
        check_vma=False,
    )
```

profile of v0, /device:TPU:0, one launch (start us, length us, event | category | flops | bytes accessed | tf_op | source)
XLA Modules:
  0.0 360.1 jit_solution(5080762425905200024)
XLA Ops:
  6.5 0.0 all-gather.2.cloned.1.call-start
  6.5 1.7 copy.27
  8.2 0.0 all-gather.2.cloned.1.call-update
  8.2 0.0 all-reduce.3.cloned.1.call-start
  8.3 0.8 copy.33
  9.1 0.1 eq.29
  9.2 0.1 eq.25
  9.3 1.3 copy.29
  10.6 0.7 broadcast_in_dim.20
  11.4 1.1 reduce-window.6
  12.5 0.2 slice_reduce_fusion
  12.8 0.1 fusion.19
  12.8 0.1 reduce_sum.44
  13.0 0.1 iota_compare_fusion
  13.1 22.5 %all-gather.2.cloned.1.call-done = bf16[1024,512]{0,1:T(8,128)(2,1)} async-done(((bf16[128,512]{0,1:T(8,128)(2,1)}), bf16[1024,512]{0,1:T(8,128)(2,1)}) %all-gather.2.cloned.1.call-update) | async-done | bytes 1048592 | tf_op jit(solution)/shard_map/all_gather | solution.py:54
  35.6 8.1 %fusion.2 = (f32[4,8,128]{2,1,0:T(8,128)S(1)}, f32[4,1024,128,8]{2,1,3,0:T(8,128)}) fusion(pred[128,1024]{0,1:T(8,128)(4,1)S(1)} %iota_compare_fusion, bf16[128,4,8,64]{0,3,2,1:T(8,128)(2,1)S(1)} %bitcast.78, bf16[1024,4,2,64]{0,3,2,1:T(8,128)(2,1)} %bitcast.80), kind=kOutput, calls=%fused_computation.7 | convolution fusion | flops 549449728 | bytes 17973248 | tf_op jit(solution)/shard_map/tgrd,ngd->grtn/dot_general | solution.py:60
  43.6 0.1 broadcast_maximum_fusion
  43.7 0.0 copy-start.1
  43.7 9.3 %fusion = f32[4,8,128]{2,1,0:T(8,128)S(1)} fusion(f32[4,1024,128,8]{2,1,3,0:T(8,128)} %get-tuple-element.12, f32[4,8,128]{2,1,0:T(8,128)S(1)} %broadcast_maximum_fusion, pred[128,1024]{0,1:T(8,128)(4,1)S(1)} %iota_compare_fusion), kind=kLoop, calls=%fused_computation.5 | loop fusion | flops 16773120 | bytes 16941056 | tf_op jit(solution)/shard_map/reduce_sum | solution.py:71
  53.0 0.1 multiply_bitcast_fusion
  53.1 0.0 copy-done.1
  53.1 7.8 %divide_convert_fusion = bf16[128,4,8,64]{0,3,2,1:T(8,128)(2,1)S(1)} fusion(f32[4,1024,128,8]{2,1,3,0:T(8,128)} %get-tuple-element.12, f32[4,8,128]{2,1,0:T(8,128)S(1)} %broadcast_maximum_fusion, pred[128,1024]{0,1:T(8,128)(4,1)S(1)} %iota_compare_fusion, bf16[1024,4,2,64]{0,3,2,1:T(8,128)(2,1)S(1)} %bitcast.81, f32[128,4,8]{0,2,1:T(8,128)S(1)} %get-tuple-element.10, ...), kind=kOutput, calls=%fused_computation.22 | convolution fusion | flops 554434560 | bytes 18006016 | tf_op jit(solution)/shard_map/grtn,ngd->grtd/dot_general | solution.py:72
  60.9 0.0 copy-start
  60.9 7.1 %convolution_convert_fusion.1 = bf16[128,2880]{0,1:T(8,128)(2,1)} fusion(bf16[2048,2880]{0,1:T(8,128)(2,1)} %param.14, bf16[128,2048]{0,1:T(8,128)(2,1)S(1)} %bitcast.85), kind=kOutput, calls=%fused_computation.12 | convolution fusion | flops 1510318080 | bytes 13058048 | tf_op jit(solution)/shard_map/dot_general | solution.py:89
  68.0 0.0 copy-start.2
  68.0 0.0 all-reduce.3.cloned.1.call-update
  68.0 0.0 reduce-scatter.4.cloned.1.call-start
  68.1 0.1 mul.93
  68.2 2.6 scatter_custom_fusion
  70.9 29.3 %all-reduce.3.cloned.1.call-done = bf16[128,2880]{0,1:T(8,128)(2,1)} async-done(((bf16[128,2880]{0,1:T(8,128)(2,1)}), bf16[128,2880]{0,1:T(8,128)(2,1)}) %all-reduce.3.cloned.1.call-update) | async-done | bytes 737296 | tf_op jit(solution)/shard_map/psum | solution.py:90
  100.2 0.0 copy-done
  100.2 2.6 convert_add_fusion
  102.8 0.0 copy-done.2
  102.8 1.6 multiply_convert_fusion
  104.4 0.3 copy.46
  104.7 0.1 concatenate.3.clone
  104.8 4.6 %gather_fusion = bf16[640,2880]{1,0:T(8,128)(2,1)} fusion(bf16[129,2880]{1,0:T(8,128)(2,1)S(1)} %concatenate.3.clone, s32[1024]{0:T(1024)S(1)} %pad_clamp_fusion.1), kind=kCustom, calls=%fused_computation | custom fusion | bytes 7375360 | tf_op jit(solution)/shard_map/gather | solution.py:95
  109.4 89.4 %all_to_all.10 = bf16[8,80,2880]{2,1,0:T(8,128)(2,1)S(1)} all-to-all(bf16[8,80,2880]{2,1,0:T(8,128)(2,1)} %bitcast.75), channel_id=1, replica_groups=mesh['groups'=2,'tok'=8,'head'=2,'pair'=1] {'tok'}, dimensions={0} | all-to-all | bytes 7372800 | tf_op jit(solution)/shard_map/all_to_all | solution.py:96
  198.8 9.5 %fusion.28 = f32[640,1440]{0,1:T(8,128)S(1)} fusion(bf16[640,2880]{1,0:T(8,128)(2,1)S(1)} %bitcast.77, bf16[2880,1440]{0,1:T(8,128)(2,1)} %bitcast.84), kind=kOutput, calls=%fused_computation.58 | convolution fusion | flops 5308416000 | bytes 15667200 | tf_op jit(solution)/shard_map/dot_general | solution.py:25
  208.3 0.5 fusion.8
  208.8 1.0 copy.37
  209.9 7.0 %convolution_convert_fusion = bf16[8,80,2880]{2,1,0:T(8,128)(2,1)} fusion(bf16[8,80,720]{2,1,0:T(8,128)(2,1)S(1)} %bitcast.79, bf16[1,720,2880]{2,1,0:T(8,128)(2,1)} %param.19), kind=kOutput, calls=%fused_computation.10 | convolution fusion | flops 2656051200 | bytes 8755200 | tf_op jit(solution)/shard_map/dot_general | solution.py:99
  216.9 8.1 %copy.42 = bf16[8,80,2880]{1,0,2:T(8,128)(2,1)} copy(bf16[8,80,2880]{2,1,0:T(8,128)(2,1)} %convolution_convert_fusion) | data formatting | bytes 7372800
  225.0 9.6 %reshape.137 = bf16[2880,640]{1,0:T(8,128)(2,1)} reshape(bf16[2880,8,80]{2,1,0:T(8,128)(2,1)} %bitcast.74) | data formatting | bytes 7372800
  234.6 0.0 reduce-scatter.4.cloned.1.call-update
  234.6 47.5 %reduce-scatter.4.cloned.1.call-done = bf16[1440,640]{1,0:T(8,128)(2,1)} async-done(((bf16[2880,640]{1,0:T(8,128)(2,1)}), bf16[1440,640]{1,0:T(8,128)(2,1)}) %reduce-scatter.4.cloned.1.call-update) | async-done | bytes 1843216
  282.1 4.8 %reshape.138 = bf16[1440,8,80]{2,1,0:T(8,128)(2,1)S(1)} reshape(bf16[1440,640]{1,0:T(8,128)(2,1)} %reduce-scatter.4.cloned.1.call-done) | data formatting | bytes 3686400
  286.9 0.0 copy-start.3
  286.9 3.5 copy.43
  290.5 4.6 %all-to-all-start.1 = ((bf16[8,80,1440]{2,1,0:T(8,128)(2,1)}), bf16[8,80,1440]{2,1,0:T(8,128)(2,1)S(1)}, u32[]{:S(2)}, u32[]{:S(2)}) async-start(bf16[8,80,1440]{2,1,0:T(8,128)(2,1)} %copy.43), calls=%async_computation.1 | async-start | bytes 3932160 | tf_op jit(solution)/shard_map/all_to_all | solution.py:105
  295.1 0.1 reshape.116
  295.2 0.0 copy-done.3
  295.2 0.1 copy.32
  295.3 46.0 %all-to-all-done.1 = bf16[8,80,1440]{2,1,0:T(8,128)(2,1)S(1)} async-done(((bf16[8,80,1440]{2,1,0:T(8,128)(2,1)}), bf16[8,80,1440]{2,1,0:T(8,128)(2,1)S(1)}, u32[]{:S(2)}, u32[]{:S(2)}) %all-to-all-start.1) | async-done | bytes 1843232 | tf_op jit(solution)/shard_map/all_to_all | solution.py:105
  341.3 3.0 gather_fusion.1
  344.2 2.9 reshape.133
  347.2 3.1 multiply_reduce_fusion
  350.2 1.4 copy.38
  351.6 1.9 add_convert_fusion
  (11 shorter events, 0.1 us)
Async XLA Ops:
  6.5 29.0 %all-gather.2.cloned.1.call-start = ((), (), s32[]{:S(2)}) async-start(), calls=%async_computation.3 | async-start | bytes 1179648 | tf_op jit(solution)/shard_map/all_gather | solution.py:54
  8.2 92.0 %all-reduce.3.cloned.1.call-start = ((), (), s32[]{:S(2)}) async-start(), calls=%async_computation.4 | async-start | bytes 1474560 | tf_op jit(solution)/shard_map/psum | solution.py:90
  43.7 9.3 %copy-start.1 = (bf16[1024,512]{0,1:T(8,128)(2,1)S(1)}, bf16[1024,512]{0,1:T(8,128)(2,1)}, u32[]{:S(2)}) copy-start(bf16[1024,512]{0,1:T(8,128)(2,1)} %all-gather.2.cloned.1.call-done) | copy-start | bytes 3145732
  60.9 39.3 %copy-start = (bf16[128,2880]{0,1:T(8,128)(2,1)S(1)}, bf16[128,2880]{0,1:T(8,128)(2,1)}, u32[]{:S(2)}) copy-start(bf16[128,2880]{0,1:T(8,128)(2,1)} %param.13) | copy-start | bytes 2211844
  68.0 34.8 %copy-start.2 = (f32[2880]{0:T(1024)S(1)}, f32[2880]{0:T(1024)}, u32[]{:S(2)}) copy-start(f32[2880]{0:T(1024)} %param.15) | copy-start | bytes 34564
  68.0 214.1 %reduce-scatter.4.cloned.1.call-start = ((), (), s32[]{:S(2)}) async-start(), calls=%async_computation.5 | async-start | bytes 5529600
  286.9 8.3 %copy-start.3 = (f32[128,4]{0,1:T(4,128)S(1)}, f32[128,4]{0,1:T(4,128)}, u32[]{:S(2)}) copy-start(f32[128,4]{0,1:T(4,128)} %param.17) | copy-start | bytes 6148
  290.5 50.8 %all-to-all-start.1 = ((bf16[8,80,1440]{2,1,0:T(8,128)(2,1)}), bf16[8,80,1440]{2,1,0:T(8,128)(2,1)S(1)}, u32[]{:S(2)}, u32[]{:S(2)}) async-start(bf16[8,80,1440]{2,1,0:T(8,128)(2,1)} %copy.43), calls=%async_computation.1 | async-start | bytes 3932160 | tf_op jit(solution)/shard_map/all_to_all | solution.py:105
Sparse Core Ops, SparseCore 0:
  8.9 26.5 all-gather.1
  68.1 32.0 all-reduce.2
  234.7 47.3 reduce-scatter.3
where the time goes:
time: 361 us; the launch traced here: 360 us
  waiting for transfers between devices  145 us (40%)
  blocking collectives  89.4 us (25%)
  local copies, waits for them, and re-layouts  47.4 us (13%)
  matrix products  39.4 us (11%)
  other arithmetic  20.5 us (6%)
  between operations  13.3 us (4%)
  starting transfers between devices  4.69 us (1%)
    all_to_all x1, blocking collectives, per_device(): lax.all_to_all(outgoing, 'tok', split_axis=0, concat_axis=0, tiled=True)  89.4 us
    unnamed x4, waiting for transfers between devices  47.5 us
    all_to_all x1, waiting for transfers between devices, per_device(): lax.all_to_all(expert_out, 'tok', split_axis=0, concat_axis=0, tiled=True)  46 us
    unnamed x17, local copies, waits for them, and re-layouts  30.3 us
    psum x1, waiting for transfers between devices, per_device(): lax.psum(partial_value.astype(jnp.bfloat16), ('head', 'pair'))  29.3 us
    all_gather x1, waiting for transfers between devices, per_device(): key_piece = lax.all_gather(keys_values, 'tok', axis=0, tiled=True)  22.5 us
    dot_general x1, matrix products, active_rows(): both = jnp.dot(flat_rows, both_columns, preferred_element_type=jnp.float32)  9.46 us
    reduce_sum x1, other arithmetic, per_device(): totals = totals * decay + jnp.sum(weights, axis=-1)  9.26 us
  transfers between devices with their start and end apart: 4, of which 4 were waited for; matrix products, arithmetic and copies ran while one was open for 2% of the time, Pallas kernels for 0%

commit v1 on v0

v1 whole, which is shorter than its diff:
```python
import functools

import jax
import jax.numpy as jnp
from jax import lax
from jax.experimental import pallas as pl
from jax.experimental.pallas import tpu as pltpu
from jax.sharding import PartitionSpec as P

HEAD_DIM = 64

MESH_ID = pl.DeviceIdType.MESH


def moe_kernel(
    dims,
    x_ref,
    gate_hbm,
    down_hbm,
    out_ref,
    gate_w,
    down_w,
    rows,
    part,
    from_core,
    kept,
    from_peer,
    hop,
    from_right,
    from_left,
    load_sem,
    row_recv,
    row_right,
    row_left,
    row_peer,
    row_core,
    part_send,
    part_recv,
    peer_send,
    peer_recv,
    hop_send,
    right_recv,
    left_recv,
):
    chips, cores, shares, pairs, width = dims
    tok = lax.axis_index("tok")
    z = tok // cores
    c = tok % cores
    mine = lax.axis_index("head") * pairs + lax.axis_index("pair")
    other = cores - 1 - c

    def tok_id(chip, core):
        return {"tok": chip * cores + core}

    def peer_id(share):
        return {"head": share // pairs, "pair": share % pairs}

    def remote(src, dst, send, recv, target):
        return pltpu.make_async_remote_copy(
            src_ref=src, dst_ref=dst, send_sem=send, recv_sem=recv,
            device_id=target, device_id_type=MESH_ID,
        )

    loads = [
        pltpu.make_async_copy(gate_hbm, gate_w, load_sem.at[0]),
        pltpu.make_async_copy(down_hbm, down_w, load_sem.at[1]),
        pltpu.make_async_copy(x_ref, rows.at[z, mine, c], load_sem.at[2]),
    ]
    for load in loads:
        load.start()

    barrier = pltpu.get_barrier_semaphore()

    @pl.when(z > 0)
    def _():
        pl.semaphore_signal(barrier, 1, device_id=tok_id(z - 1, c), device_id_type=MESH_ID)

    @pl.when(z < chips - 1)
    def _():
        pl.semaphore_signal(barrier, 1, device_id=tok_id(z + 1, c), device_id_type=MESH_ID)

    if cores > 1:
        pl.semaphore_signal(barrier, 1, device_id=tok_id(z, other), device_id_type=MESH_ID)
    for d in range(1, shares):
        pl.semaphore_signal(
            barrier, 1, device_id=peer_id((mine + d) % shares), device_id_type=MESH_ID
        )
    sides = jnp.where(z > 0, 1, 0) + jnp.where(z < chips - 1, 1, 0)
    pl.semaphore_wait(barrier, sides + (cores - 1) + (shares - 1))
    loads[2].wait()

    near = jnp.minimum(z, chips - 1 - z)

    def chip_at(i):
        inner = jnp.where(i % 2 == 1, z - (i + 1) // 2, z + i // 2)
        outer = jnp.where(z < chips - 1 - z, i, chips - 1 - i)
        return jnp.where(i <= 2 * near, inner, outer)

    def row_copy(chip, share, core, send, target):
        slot = rows.at[chip, share, core]
        return remote(slot, slot, send, row_recv.at[chip, core, share], target)

    def go_right(chip):
        return (chip <= z) & (z < chips - 1)

    def go_left(chip):
        return (chip >= z) & (z > 0)

    def right_copy(chip):
        return row_copy(chip, mine, c, row_right.at[chip], tok_id(z + 1, c))

    def left_copy(chip):
        return row_copy(chip, mine, c, row_left.at[chip], tok_id(z - 1, c))

    def peer_copy(chip, d):
        return row_copy(chip, mine, c, row_peer.at[chip, d - 1], peer_id((mine + d) % shares))

    def core_copy(chip, share):
        return row_copy(chip, share, c, row_core.at[chip, share], tok_id(z, other))

    def row_wait(chip, share, core):
        slot = rows.at[chip, share, core]
        pltpu.make_async_copy(slot, slot, row_recv.at[chip, core, share]).wait()

    def forward(i):
        chip = chip_at(i)

        @pl.when(go_right(chip))
        def _():
            right_copy(chip).start()

        @pl.when(go_left(chip))
        def _():
            left_copy(chip).start()

        for d in range(1, shares):
            peer_copy(chip, d).start()
        if cores > 1:
            core_copy(chip, mine).start()

    forward(0)
    loads[0].wait()
    loads[1].wait()

    tail = (width // 128) * 128
    wide = rows.shape[-1]
    depth = rows.shape[-2]
    experts = chips * cores
    tail_lane = tail + lax.broadcasted_iota(jnp.int32, (cores * depth, wide - tail), 1)
    weight_lane = (tail_lane == width + tok) | (tail_lane == width + experts + tok)

    def kept_at(chip, share):
        return kept.at[chip, share] if cores > 1 else part.at[chip, share, 0]

    def part_copy(chip, share):
        return remote(
            part.at[chip, share, other], from_core.at[chip, share],
            part_send.at[chip, share], part_recv.at[chip, share], tok_id(z, other),
        )

    def sum_copy(chip, d):
        share = (mine + d) % shares
        return remote(
            kept_at(chip, share), from_peer.at[chip, mine],
            peer_send.at[chip, d - 1], peer_recv.at[chip, mine], peer_id(share),
        )

    def compute(i, carry):
        @pl.when(i + 1 < chips)
        def _():
            row_wait(chip_at(i + 1), mine, c)
            forward(i + 1)

        chip = chip_at(i)
        for d in range(1, shares):
            share = (mine + d) % shares
            row_wait(chip, share, c)
            if cores > 1:
                core_copy(chip, share).start()
        if cores > 1:
            for share in range(shares):
                row_wait(chip, share, other)
        gate = jnp.zeros((cores * depth, gate_w.shape[-1]), jnp.float32)
        up = gate
        for share in range(shares):
            block = rows[chip, share].reshape(cores * depth, wide)
            gate += jnp.dot(block, gate_w[0, share], preferred_element_type=jnp.float32)
            up += jnp.dot(block, gate_w[1, share], preferred_element_type=jnp.float32)
        active = (gate * jax.nn.sigmoid(1.702 * gate) * (up + 1.0)).astype(jnp.bfloat16)
        ends = rows[chip, 0, :, :, tail:].reshape(cores * depth, wide - tail).astype(jnp.float32)
        weight = jnp.sum(jnp.where(weight_lane, ends, 0.0), axis=1, keepdims=True)
        for share in range(shares):
            out = jnp.dot(active, down_w[share], preferred_element_type=jnp.float32)
            out = (out * weight).astype(jnp.bfloat16)
            part[chip, share] = out.reshape(cores, depth, width)
            if cores > 1:
                part_copy(chip, share).start()
        for share in range(shares):
            if cores > 1:
                part_copy(chip, share).wait_recv()
                total = part[chip, share, c].astype(jnp.float32)
                total += from_core[chip, share].astype(jnp.float32)
                kept[chip, share] = total.astype(jnp.bfloat16)
        for d in range(1, shares):
            sum_copy(chip, d).start()
        return carry

    lax.fori_loop(0, chips, compute, 0)

    def right_hop(chip):
        return remote(
            hop.at[chip], from_left.at[chip], hop_send.at[chip], left_recv.at[chip],
            tok_id(z + 1, c),
        )

    def left_hop(chip):
        return remote(
            hop.at[chip], from_right.at[chip], hop_send.at[chip], right_recv.at[chip],
            tok_id(z - 1, c),
        )

    def hop_wait(buffer, sem, chip):
        pltpu.make_async_copy(buffer.at[chip], buffer.at[chip], sem.at[chip]).wait()

    def give_back(j, carry):
        chip = chip_at(chips - 1 - j)
        total = kept_at(chip, mine)[...].astype(jnp.float32)
        for d in range(1, shares):
            share = (mine + d) % shares
            slot = from_peer.at[chip, share]
            pltpu.make_async_copy(slot, slot, peer_recv.at[chip, share]).wait()
            total += from_peer[chip, share].astype(jnp.float32)
        out_ref[...] = total

        @pl.when((chip <= z) & (z < chips - 1))
        def _():
            hop_wait(from_right, right_recv, chip)
            out_ref[...] += from_right[chip].astype(jnp.float32)

        @pl.when((chip >= z) & (z > 0))
        def _():
            hop_wait(from_left, left_recv, chip)
            out_ref[...] += from_left[chip].astype(jnp.float32)

        @pl.when(chip != z)
        def _():
            hop[chip] = out_ref[...].astype(jnp.bfloat16)

        @pl.when(chip < z)
        def _():
            left_hop(chip).start()

        @pl.when(chip > z)
        def _():
            right_hop(chip).start()

        return carry

    lax.fori_loop(0, chips, give_back, 0)

    def drain(chip, carry):
        @pl.when(go_right(chip))
        def _():
            right_copy(chip).wait_send()

        @pl.when(go_left(chip))
        def _():
            left_copy(chip).wait_send()

        for d in range(1, shares):
            peer_copy(chip, d).wait_send()
            sum_copy(chip, d).wait_send()
        if cores > 1:
            for share in range(shares):
                core_copy(chip, share).wait_send()
                part_copy(chip, share).wait_send()

        @pl.when(chip < z)
        def _():
            left_hop(chip).wait_send()

        @pl.when(chip > z)
        def _():
            right_hop(chip).wait_send()

        return carry

    lax.fori_loop(0, chips, drain, 0)


def moe(dims, own_rows, gate_w, down_w):
    chips, cores, shares, pairs, width = dims
    depth, wide = own_rows.shape
    hidden = down_w.shape[1]
    bf16 = jnp.bfloat16
    dma = pltpu.SemaphoreType.DMA
    return pl.pallas_call(
        functools.partial(moe_kernel, dims),
        out_shape=jax.ShapeDtypeStruct((depth, width), jnp.float32),
        in_specs=[
            pl.BlockSpec(memory_space=pltpu.VMEM),
            pl.BlockSpec(memory_space=pl.ANY),
            pl.BlockSpec(memory_space=pl.ANY),
        ],
        out_specs=pl.BlockSpec(memory_space=pltpu.VMEM),
        scratch_shapes=[
            pltpu.VMEM(gate_w.shape, bf16),
            pltpu.VMEM(down_w.shape, bf16),
            pltpu.VMEM((chips, shares, cores, depth, wide), bf16),
            pltpu.VMEM((chips, shares, cores, depth, width), bf16),
            pltpu.VMEM((chips, shares, depth, width) if cores > 1 else (8, 128), bf16),
            pltpu.VMEM((chips, shares, depth, width) if cores > 1 else (8, 128), bf16),
            pltpu.VMEM((chips, shares, depth, width), bf16),
            pltpu.VMEM((chips, depth, width), bf16),
            pltpu.VMEM((chips, depth, width), bf16),
            pltpu.VMEM((chips, depth, width), bf16),
            dma((3,)),
            dma((chips, cores, shares)),
            dma((chips,)),
            dma((chips,)),
            dma((chips, max(shares - 1, 1))),
            dma((chips, shares)),
            dma((chips, shares)),
            dma((chips, shares)),
            dma((chips, max(shares - 1, 1))),
            dma((chips, shares)),
            dma((chips,)),
            dma((chips,)),
            dma((chips,)),
        ],
        compiler_params=pltpu.CompilerParams(
            collective_id=0, has_side_effects=True, vmem_limit_bytes=60 * 1024 * 1024
        ),
        cost_estimate=pl.CostEstimate(
            flops=6 * chips * cores * depth * shares * width * hidden,
            bytes_accessed=6 * shares * width * hidden,
            transcendentals=0,
        ),
    )(own_rows, gate_w, down_w)


def per_device(
    queries,
    keys_values,
    sink_logits,
    residual,
    out_weight,
    norm_gain,
    expert_ids,
    route_weights,
    gate_up,
    down_weight,
):
    tok_rows = queries.shape[0]
    kv_groups = keys_values.shape[1] // (2 * HEAD_DIM)
    local_heads = queries.shape[1] // HEAD_DIM
    repeat = local_heads // kv_groups
    position = lax.axis_index("tok") * tok_rows + jnp.arange(tok_rows, dtype=jnp.int32)
    grouped = queries.reshape(tok_rows, kv_groups, repeat, HEAD_DIM)
    start_max = jnp.broadcast_to(
        sink_logits.reshape(kv_groups, repeat)[:, :, None], (kv_groups, repeat, tok_rows)
    )
    start_totals = jnp.ones((kv_groups, repeat, tok_rows), jnp.float32)
    start_accum = jnp.zeros((kv_groups, repeat, tok_rows, HEAD_DIM), jnp.float32)
    key_piece = lax.all_gather(keys_values, "tok", axis=0, tiled=True)
    totals = start_totals
    accum = start_accum
    count = key_piece.shape[0]
    split_piece = key_piece.reshape(count, kv_groups, 2, HEAD_DIM)
    scores = (
        jnp.einsum(
            "tgrd,ngd->grtn", grouped, split_piece[:, :, 0], preferred_element_type=jnp.float32
        )
        * 0.125
    )
    key_position = jnp.arange(count, dtype=jnp.int32)
    allowed = key_position[None, :] <= position[:, None]
    scores = jnp.where(allowed, scores, jnp.float32(-1e30))
    new_max = jnp.maximum(start_max, jnp.max(scores, axis=-1))
    decay = jnp.exp(start_max - new_max)
    weights = jnp.exp(scores - new_max[..., None])
    totals = totals * decay + jnp.sum(weights, axis=-1)
    update = jnp.einsum(
        "grtn,ngd->grtd",
        weights.astype(jnp.bfloat16),
        split_piece[:, :, 1],
        preferred_element_type=jnp.float32,
    )
    accum = accum * decay[..., None] + update
    final_max, totals, accum = (new_max, totals, accum)
    attended = (accum / totals[..., None]).astype(jnp.bfloat16)
    attended = jnp.transpose(attended, (2, 0, 1, 3)).reshape(tok_rows, local_heads * HEAD_DIM)
    width = out_weight.shape[1]
    share = width // lax.axis_size(("head", "pair"))
    column_start = lax.axis_index(("head", "pair")) * share
    partial_value = jnp.dot(attended, out_weight, preferred_element_type=jnp.float32)
    projected = lax.psum(partial_value.astype(jnp.bfloat16), ("head", "pair")).astype(jnp.float32)
    stream = residual.astype(jnp.float32) + projected
    inverse = lax.rsqrt(jnp.mean(stream * stream, axis=-1, keepdims=True) + 1e-05)
    normed = (stream * inverse * norm_gain).astype(jnp.bfloat16)
    experts = lax.axis_size("tok")
    pairs = lax.axis_size("pair")
    cores = 2 // pairs
    shares = width // share
    hidden = down_weight.shape[1]
    wide = -(-(share + 2 * experts) // 128) * 128
    expert = jnp.arange(experts, dtype=jnp.int32)
    routed = expert_ids[:, :, None] == expert
    dense = jnp.sum(jnp.where(routed, route_weights[:, :, None], 0.0), axis=1)
    high = lax.reduce_precision(dense, 8, 7)
    own_rows = jnp.concatenate(
        [
            lax.dynamic_slice_in_dim(normed, column_start, share, 1),
            high.astype(jnp.bfloat16),
            (dense - high).astype(jnp.bfloat16),
            jnp.zeros((tok_rows, wide - share - 2 * experts), jnp.bfloat16),
        ],
        axis=1,
    )
    gate_w = jnp.transpose(gate_up[0], (1, 0, 2)).reshape(2, shares, share, hidden)
    gate_w = jnp.pad(gate_w, ((0, 0), (0, 0), (0, wide - share), (0, 0)))
    down_w = jnp.transpose(down_weight[0].reshape(hidden, shares, share), (1, 0, 2))
    stream_share = lax.dynamic_slice_in_dim(stream, column_start, share, 1)
    mixture = moe((experts // cores, cores, shares, pairs, share), own_rows, gate_w, down_w)
    return (stream_share + mixture).astype(jnp.bfloat16)


def solution(mesh):
    placed = (
        P(("groups", "tok"), ("head", "pair")),
        P(("groups", "tok"), ("head", "pair")),
        P(("head", "pair")),
        P(("groups", "tok"), None),
        P(("head", "pair"), None),
        P(),
        P(("groups", "tok"), None),
        P(("groups", "tok"), None),
        P("tok", None, None, ("head", "pair")),
        P("tok", ("head", "pair"), None),
    )
    return jax.shard_map(
        per_device,
        mesh=mesh,
        in_specs=placed,
        out_specs=P(("groups", "tok"), ("head", "pair")),
        check_vma=False,
    )
```

time: 361 us -> 216 us (0.60)
  waiting for transfers between devices: 145 us -> 25.2 us
  Pallas kernels: 0 us -> 102 us
  blocking collectives: 89.4 us -> 0 us
  matrix products: 39.4 us -> 19.4 us
  other arithmetic: 20.5 us -> 12.7 us
  local copies, waits for them, and re-layouts: 47.4 us -> 41.7 us
  starting transfers between devices: 4.69 us -> 0.04 us
    pallas_call x0 -> x1, Pallas kernels: none -> 102 us  [moe(): pl.pallas_call(functools.partial(moe_kernel, dims), out_shape=jax.ShapeDt...]
    all_to_all x1 -> x0, blocking collectives: 89.4 us -> none  [per_device(): lax.all_to_all(outgoing, 'tok', split_axis=0, concat_axis=0, tiled=True)]
    unnamed x4 -> x2, waiting for transfers between devices: 47.5 us -> 0.03 us
    all_to_all x1 -> x0, waiting for transfers between devices: 46 us -> none  [per_device(): lax.all_to_all(expert_out, 'tok', split_axis=0, concat_axis=0, tiled=True)]
    psum x1, waiting for transfers between devices: 29.3 us -> 0.02 us  [per_device(): lax.psum(partial_value.astype(jnp.bfloat16), ('head', 'pair'))]
    unnamed x17 -> x20, local copies, waits for them, and re-layouts: 30.3 us -> 11 us
    dot_general x2 -> x0, matrix products: 16.5 us -> none  [the longest x1 9.46 us: active_rows(): both = jnp.dot(flat_rows, both_columns, preferred_element_type=jnp.float32)]
    transpose x0 -> x1, local copies, waits for them, and re-layouts: none -> 12 us  [per_device(): jnp.transpose(gate_up[0], (1, 0, 2)).reshape(2, shares, share, hidden)]
  transfers between devices with their start and end apart: 4 -> 2, of which waited for: 4 -> 1; matrix products, arithmetic and copies ran while one was open for 2% -> 17% of each run, Pallas kernels for 0% -> 0%
where the time goes in v1:
time: 216 us; the launch traced here: 215 us
  Pallas kernels  102 us (47%)
  local copies, waits for them, and re-layouts  41.7 us (19%)
  waiting for transfers between devices  25.2 us (12%)
  matrix products  19.4 us (9%)
  between operations  13.6 us (6%)
  other arithmetic  12.7 us (6%)
    pallas_call x1, Pallas kernels, moe(): pl.pallas_call(functools.partial(moe_kernel, dims), out_shape=jax.ShapeDt...  102 us
    all_gather x1, waiting for transfers between devices, per_device(): key_piece = lax.all_gather(keys_values, 'tok', axis=0, tiled=True)  25.1 us
    transpose x1, local copies, waits for them, and re-layouts, per_device(): jnp.transpose(gate_up[0], (1, 0, 2)).reshape(2, shares, share, hidden)  12 us
    unnamed x20, local copies, waits for them, and re-layouts  11 us
    reduce_sum x1, other arithmetic, per_device(): totals = totals * decay + jnp.sum(weights, axis=-1)  9.3 us
    dot_general x1, matrix products, per_device(): jnp.einsum('tgrd,ngd->grtn', grouped, split_piece[:, :, 0], preferred_ele...  8.15 us
    pad x1, local copies, waits for them, and re-layouts, per_device(): gate_w = jnp.pad(gate_w, ((0, 0), (0, 0), (0, wide - share), (0, 0)))  8.02 us
    dot_general x1, matrix products, per_device(): jnp.einsum('grtn,ngd->grtd', weights.astype(jnp.bfloat16), split_piece[:,...  7.97 us
  transfers between devices with their start and end apart: 2, of which 1 were waited for; matrix products, arithmetic and copies ran while one was open for 17% of the time, Pallas kernels for 0%

profile of v1, /device:TPU:0, one launch (start us, length us, event | category | flops | bytes accessed | tf_op | source)
XLA Modules:
  0.0 214.6 jit_solution(7982907568753178154)
XLA Ops:
  6.5 0.0 all-gather.2.cloned.1.call-start
  6.5 1.7 copy.46
  8.2 0.0 all-gather.2.cloned.1.call-update
  8.2 0.0 all-reduce.3.cloned.1.call-start
  8.3 1.3 copy.48
  9.6 0.7 broadcast_in_dim.43
  10.3 0.1 iota_compare_fusion
  10.4 25.1 %all-gather.2.cloned.1.call-done = bf16[1024,512]{0,1:T(8,128)(2,1)} async-done(((bf16[128,512]{0,1:T(8,128)(2,1)}), bf16[1024,512]{0,1:T(8,128)(2,1)}) %all-gather.2.cloned.1.call-update) | async-done | bytes 1048592 | tf_op jit(solution)/shard_map/all_gather | solution.py:365
  35.6 0.0 copy-start.1
  35.6 8.2 %fusion.2 = (f32[4,8,128]{2,1,0:T(8,128)S(1)}, f32[4,1024,128,8]{2,1,3,0:T(8,128)}) fusion(pred[128,1024]{0,1:T(8,128)(4,1)S(1)} %iota_compare_fusion, bf16[128,4,8,64]{0,3,2,1:T(8,128)(2,1)S(1)} %bitcast.59, bf16[1024,4,2,64]{0,3,2,1:T(8,128)(2,1)} %bitcast.60), kind=kOutput, calls=%fused_computation.4 | convolution fusion | flops 549449728 | bytes 17973248 | tf_op jit(solution)/shard_map/tgrd,ngd->grtn/dot_general | solution.py:371
  43.7 0.1 broadcast_maximum_fusion
  43.8 9.3 %fusion = f32[4,8,128]{2,1,0:T(8,128)S(1)} fusion(f32[4,1024,128,8]{2,1,3,0:T(8,128)} %get-tuple-element.12, f32[4,8,128]{2,1,0:T(8,128)S(1)} %broadcast_maximum_fusion, pred[128,1024]{0,1:T(8,128)(4,1)S(1)} %iota_compare_fusion), kind=kLoop, calls=%fused_computation.2 | loop fusion | flops 16773120 | bytes 16941056 | tf_op jit(solution)/shard_map/reduce_sum | solution.py:382
  53.1 0.0 slice-start
  53.1 0.1 multiply_bitcast_fusion
  53.2 0.0 copy-done.1
  53.2 0.0 slice-start.1
  53.2 0.0 slice-start.2
  53.2 0.0 copy-start
  53.2 8.0 %divide_convert_fusion = bf16[128,4,8,64]{0,3,2,1:T(8,128)(2,1)S(1)} fusion(f32[4,1024,128,8]{2,1,3,0:T(8,128)} %get-tuple-element.12, f32[4,8,128]{2,1,0:T(8,128)S(1)} %broadcast_maximum_fusion, pred[128,1024]{0,1:T(8,128)(4,1)S(1)} %iota_compare_fusion, bf16[1024,4,2,64]{0,3,2,1:T(8,128)(2,1)S(1)} %bitcast.61, f32[128,4,8]{0,2,1:T(8,128)S(1)} %get-tuple-element.8, ...), kind=kOutput, calls=%fused_computation.12 | convolution fusion | flops 554434560 | bytes 18006016 | tf_op jit(solution)/shard_map/grtn,ngd->grtd/dot_general | solution.py:383
  61.2 0.0 copy-start.3
  61.2 0.0 copy-start.4
  61.2 0.0 slice-done
  61.2 0.1 slice-done.1
  61.4 1.0 slice-done.2
  62.3 3.2 %convolution_convert_fusion = bf16[128,2880]{0,1:T(8,128)(2,1)S(1)} fusion(bf16[2048,2880]{0,1:T(8,128)(2,1)S(1)} %bitcast.63, bf16[128,2048]{0,1:T(8,128)(2,1)S(1)} %bitcast.64), kind=kOutput, calls=%fused_computation.7 | convolution fusion | flops 1510318080 | bytes 13058048 | tf_op jit(solution)/shard_map/dot_general | solution.py:396
  65.6 1.2 copy.51
  66.7 0.0 all-reduce.3.cloned.1.call-update
  66.8 0.0 copy-done
  66.8 0.3 copy.45
  67.1 0.0 copy-done.3
  67.1 0.0 copy-done.4
  67.2 0.1 copy.52
  67.3 0.1 copy.53
  67.4 0.1 copy.54
  67.5 0.0 copy-start.2
  67.5 12.0 %copy.55 = bf16[2,2880,720]{2,1,0:T(8,128)(2,1)} copy(bf16[2,2880,720]{1,2,0:T(8,128)(2,1)} %bitcast.57) | data formatting | bytes 16588800 | tf_op jit(solution)/shard_map/transpose | solution.py:420
  79.5 6.6 %copy.56 = bf16[1,720,2880]{1,2,0:T(8,128)(2,1)} copy(bf16[1,720,2880]{2,1,0:T(8,128)(2,1)} %param.19) | data formatting | bytes 8294400 | tf_op args[9]
  86.1 6.5 %copy.57 = bf16[720,2,1440]{2,0,1:T(8,128)(2,1)} copy(bf16[720,2,1440]{0,2,1:T(8,128)(2,1)} %bitcast.56) | data formatting | bytes 8294400 | tf_op jit(solution)/shard_map/reshape;squeeze | solution.py:422
  92.6 0.0 copy-done.2
  92.6 0.1 dynamic-slice
  92.7 8.0 %pad.4.gate_hbm = bf16[2,2,1536,720]{3,2,1,0:T(8,128)(2,1)} pad(bf16[2,2,1440,720]{3,2,1,0:T(8,128)(2,1)} %bitcast.55, bf16[]{:T(256)} %constant.34.clone.1), padding=0_0x0_0x0_96x0_0 | pad | bytes 17141762 | tf_op jit(solution)/shard_map/jit(_pad)/pad | solution.py:421
  100.7 0.0 all-reduce.3.cloned.1.call-done
  100.7 1.5 multiply_reduce_fusion
  102.2 0.3 multiply_convert_fusion
  102.5 0.9 concatenate.3.x_ref
  103.4 102.0 %shard_map.100 = f32[128,1440]{1,0:T(8,128)} custom-call(bf16[128,1536]{1,0:T(8,128)(2,1)} %concatenate.3.x_ref, bf16[2,2,1536,720]{3,2,1,0:T(8,128)(2,1)} %pad.4.gate_hbm, bf16[2,720,1440]{2,1,0:T(8,128)(2,1)} %bitcast.58), custom_call_target="tpu_custom_call" | custom-call | flops 12740198400 | bytes 12441600 | tf_op jit(solution)/shard_map/pallas_call | solution.py:297
  205.4 1.4 add_convert_fusion
  206.8 0.9 copy.58
  (7 shorter events, 0.0 us)
Async XLA Ops:
  6.5 29.0 %all-gather.2.cloned.1.call-start = ((), (), s32[]{:S(2)}) async-start(), calls=%async_computation | async-start | bytes 1179648 | tf_op jit(solution)/shard_map/all_gather | solution.py:365
  8.2 92.5 %all-reduce.3.cloned.1.call-start = ((), (), s32[]{:S(2)}) async-start(), calls=%async_computation.1 | async-start | bytes 1507328 | tf_op jit(solution)/shard_map/psum | solution.py:397
  35.6 17.6 %copy-start.1 = (bf16[1024,512]{0,1:T(8,128)(2,1)S(1)}, bf16[1024,512]{0,1:T(8,128)(2,1)}, u32[]{:S(2)}) copy-start(bf16[1024,512]{0,1:T(8,128)(2,1)} %all-gather.2.cloned.1.call-done) | copy-start | bytes 3145732
  53.1 8.2 %slice-start = ((s8[11796480]{0:T(1024)(128)(4,1)}), s8[4194304]{0:T(1024)(128)(4,1)S(1)}, s32[]{:S(2)}) async-start(s8[11796480]{0:T(1024)(128)(4,1)} %bitcast.62), calls=%async_computation.2 | async-start | bytes 8388608
  53.2 8.2 %slice-start.1 = ((s8[11796480]{0:T(1024)(128)(4,1)}), s8[4194304]{0:T(1024)(128)(4,1)S(1)}, s32[]{:S(2)}) async-start(s8[11796480]{0:T(1024)(128)(4,1)} %bitcast.62), calls=%async_computation.3 | async-start | bytes 8388608
  53.2 9.1 %slice-start.2 = ((s8[11796480]{0:T(1024)(128)(4,1)}), s8[3407872]{0:T(1024)(128)(4,1)S(1)}, s32[]{:S(2)}) async-start(s8[11796480]{0:T(1024)(128)(4,1)} %bitcast.62), calls=%async_computation.4 | async-start | bytes 6815744
  53.2 13.5 %copy-start = (bf16[128,2880]{0,1:T(8,128)(2,1)S(1)}, bf16[128,2880]{0,1:T(8,128)(2,1)}, u32[]{:S(2)}) copy-start(bf16[128,2880]{0,1:T(8,128)(2,1)} %param.13) | copy-start | bytes 2211844
  61.2 5.9 %copy-start.3 = (f32[128,4]{0,1:T(4,128)S(1)}, f32[128,4]{0,1:T(4,128)}, u32[]{:S(2)}) copy-start(f32[128,4]{0,1:T(4,128)} %param.17) | copy-start | bytes 6148
  61.2 5.9 %copy-start.4 = (s32[128,4]{0,1:T(4,128)S(1)}, s32[128,4]{0,1:T(4,128)}, u32[]{:S(2)}) copy-start(s32[128,4]{0,1:T(4,128)} %param.16) | copy-start | bytes 6148
  67.5 25.1 %copy-start.2 = (f32[2880]{0:T(1024)S(1)}, f32[2880]{0:T(1024)}, u32[]{:S(2)}) copy-start(f32[2880]{0:T(1024)} %param.15) | copy-start | bytes 34564
Sparse Core Ops, SparseCore 0:
  8.9 26.5 all-gather.1
  66.9 32.4 all-reduce.2

commit v2 on v1

--- a/solution.py
+++ b/solution.py
@@ -14,7 +14,10 @@
 
 def moe_kernel(
     dims,
-    x_ref,
+    parts_ref,
+    residual_ref,
+    gain_ref,
+    tail_ref,
     gate_hbm,
     down_hbm,
     out_ref,
@@ -28,6 +31,15 @@
     hop,
     from_right,
     from_left,
+    peer_parts,
+    stream,
+    squares,
+    peer_squares,
+    acc,
+    parts_send,
+    parts_recv,
+    squares_send,
+    squares_recv,
     load_sem,
     row_recv,
     row_right,
@@ -62,9 +74,8 @@
         )
 
     loads = [
-        pltpu.make_async_copy(gate_hbm, gate_w, load_sem.at[0]),
+        pltpu.make_async_copy(gate_hbm, gate_w.at[:, :, pl.ds(0, width)], load_sem.at[0]),
         pltpu.make_async_copy(down_hbm, down_w, load_sem.at[1]),
-        pltpu.make_async_copy(x_ref, rows.at[z, mine, c], load_sem.at[2]),
     ]
     for load in loads:
         load.start()
@@ -87,7 +98,45 @@
         )
     sides = jnp.where(z > 0, 1, 0) + jnp.where(z < chips - 1, 1, 0)
     pl.semaphore_wait(barrier, sides + (cores - 1) + (shares - 1))
-    loads[2].wait()
+
+    def parts_copy(d):
+        share = (mine + d) % shares
+        return remote(
+            parts_ref.at[share], peer_parts.at[mine], parts_send.at[d - 1],
+            parts_recv.at[mine], peer_id(share),
+        )
+
+    def squares_copy(d):
+        return remote(
+            squares, peer_squares.at[mine], squares_send.at[d - 1],
+            squares_recv.at[mine], peer_id((mine + d) % shares),
+        )
+
+    for d in range(1, shares):
+        parts_copy(d).start()
+    gate_w[:, :, width:, :] = jnp.zeros(
+        gate_w.shape[:2] + (gate_w.shape[2] - width, gate_w.shape[3]), jnp.bfloat16
+    )
+    stream[...] = residual_ref[...].astype(jnp.float32) + parts_ref[mine].astype(jnp.float32)
+    for d in range(1, shares):
+        share = (mine + d) % shares
+        slot = peer_parts.at[share]
+        pltpu.make_async_copy(slot, slot, parts_recv.at[share]).wait()
+        stream[...] += peer_parts[share].astype(jnp.float32)
+    own = stream[...]
+    square = jnp.sum(own * own, axis=1, keepdims=True)
+    squares[...] = jnp.broadcast_to(square, squares.shape)
+    for d in range(1, shares):
+        squares_copy(d).start()
+    total_square = squares[...]
+    for d in range(1, shares):
+        share = (mine + d) % shares
+        slot = peer_squares.at[share]
+        pltpu.make_async_copy(slot, slot, squares_recv.at[share]).wait()
+        total_square += peer_squares[share]
+    inverse = lax.rsqrt(total_square[:, :1] / (shares * width) + 1e-05)
+    normed = stream[...] * inverse * gain_ref[...] + tail_ref[...].astype(jnp.float32)
+    rows[z, mine, c] = normed.astype(jnp.bfloat16)
 
     near = jnp.minimum(z, chips - 1 - z)
 
@@ -230,21 +279,25 @@
             slot = from_peer.at[chip, share]
             pltpu.make_async_copy(slot, slot, peer_recv.at[chip, share]).wait()
             total += from_peer[chip, share].astype(jnp.float32)
-        out_ref[...] = total
+        acc[...] = total
 
         @pl.when((chip <= z) & (z < chips - 1))
         def _():
             hop_wait(from_right, right_recv, chip)
-            out_ref[...] += from_right[chip].astype(jnp.float32)
+            acc[...] += from_right[chip].astype(jnp.float32)
 
         @pl.when((chip >= z) & (z > 0))
         def _():
             hop_wait(from_left, left_recv, chip)
-            out_ref[...] += from_left[chip].astype(jnp.float32)
+            acc[...] += from_left[chip].astype(jnp.float32)
+
+        @pl.when(chip == z)
+        def _():
+            out_ref[...] = (stream[:, :width] + acc[...]).astype(jnp.bfloat16)
 
         @pl.when(chip != z)
         def _():
-            hop[chip] = out_ref[...].astype(jnp.bfloat16)
+            hop[chip] = acc[...].astype(jnp.bfloat16)
 
         @pl.when(chip < z)
         def _():
@@ -286,25 +339,28 @@
         return carry
 
     lax.fori_loop(0, chips, drain, 0)
-
-
-def moe(dims, own_rows, gate_w, down_w):
+    for d in range(1, shares):
+        parts_copy(d).wait_send()
+        squares_copy(d).wait_send()
+
+
+def moe(dims, parts, residual, gain, tail, gate_w, down_w):
     chips, cores, shares, pairs, width = dims
-    depth, wide = own_rows.shape
+    depth, wide = residual.shape
     hidden = down_w.shape[1]
     bf16 = jnp.bfloat16
     dma = pltpu.SemaphoreType.DMA
     return pl.pallas_call(
         functools.partial(moe_kernel, dims),
-        out_shape=jax.ShapeDtypeStruct((depth, width), jnp.float32),
-        in_specs=[
-            pl.BlockSpec(memory_space=pltpu.VMEM),
+        out_shape=jax.ShapeDtypeStruct((depth, width), jnp.bfloat16),
+        in_specs=[pl.BlockSpec(memory_space=pltpu.VMEM)] * 4
+        + [
             pl.BlockSpec(memory_space=pl.ANY),
             pl.BlockSpec(memory_space=pl.ANY),
         ],
         out_specs=pl.BlockSpec(memory_space=pltpu.VMEM),
         scratch_shapes=[
-            pltpu.VMEM(gate_w.shape, bf16),
+            pltpu.VMEM((2, shares, wide, hidden), bf16),
             pltpu.VMEM(down_w.shape, bf16),
             pltpu.VMEM((chips, shares, cores, depth, wide), bf16),
             pltpu.VMEM((chips, shares, cores, depth, width), bf16),
@@ -314,7 +370,16 @@
             pltpu.VMEM((chips, depth, width), bf16),
             pltpu.VMEM((chips, depth, width), bf16),
             pltpu.VMEM((chips, depth, width), bf16),
-            dma((3,)),
+            pltpu.VMEM((shares, depth, wide), bf16),
+            pltpu.VMEM((depth, wide), jnp.float32),
+            pltpu.VMEM((depth, 128), jnp.float32),
+            pltpu.VMEM((shares, depth, 128), jnp.float32),
+            pltpu.VMEM((depth, width), jnp.float32),
+            dma((max(shares - 1, 1),)),
+            dma((shares,)),
+            dma((max(shares - 1, 1),)),
+            dma((shares,)),
+            dma((2,)),
             dma((chips, cores, shares)),
             dma((chips,)),
             dma((chips,)),
@@ -336,7 +401,7 @@
             bytes_accessed=6 * shares * width * hidden,
             transcendentals=0,
         ),
-    )(own_rows, gate_w, down_w)
+    )(parts, residual, gain, tail, gate_w, down_w)
 
 
 def per_device(
@@ -363,6 +428,12 @@
     start_totals = jnp.ones((kv_groups, repeat, tok_rows), jnp.float32)
     start_accum = jnp.zeros((kv_groups, repeat, tok_rows, HEAD_DIM), jnp.float32)
     key_piece = lax.all_gather(keys_values, "tok", axis=0, tiled=True)
+    hidden = down_weight.shape[1]
+    shares = lax.axis_size(("head", "pair"))
+    share = out_weight.shape[1] // shares
+    gate_w = jnp.transpose(gate_up[0], (1, 0, 2)).reshape(2, shares, share, hidden)
+    down_w = jnp.transpose(down_weight[0].reshape(hidden, shares, share), (1, 0, 2))
+    key_piece, gate_w, down_w = lax.optimization_barrier((key_piece, gate_w, down_w))
     totals = start_totals
     accum = start_accum
     count = key_piece.shape[0]
@@ -394,35 +465,30 @@
     share = width // lax.axis_size(("head", "pair"))
     column_start = lax.axis_index(("head", "pair")) * share
     partial_value = jnp.dot(attended, out_weight, preferred_element_type=jnp.float32)
-    projected = lax.psum(partial_value.astype(jnp.bfloat16), ("head", "pair")).astype(jnp.float32)
-    stream = residual.astype(jnp.float32) + projected
-    inverse = lax.rsqrt(jnp.mean(stream * stream, axis=-1, keepdims=True) + 1e-05)
-    normed = (stream * inverse * norm_gain).astype(jnp.bfloat16)
     experts = lax.axis_size("tok")
     pairs = lax.axis_size("pair")
     cores = 2 // pairs
     shares = width // share
-    hidden = down_weight.shape[1]
     wide = -(-(share + 2 * experts) // 128) * 128
     expert = jnp.arange(experts, dtype=jnp.int32)
     routed = expert_ids[:, :, None] == expert
     dense = jnp.sum(jnp.where(routed, route_weights[:, :, None], 0.0), axis=1)
     high = lax.reduce_precision(dense, 8, 7)
-    own_rows = jnp.concatenate(
-        [
-            lax.dynamic_slice_in_dim(normed, column_start, share, 1),
-            high.astype(jnp.bfloat16),
-            (dense - high).astype(jnp.bfloat16),
-            jnp.zeros((tok_rows, wide - share - 2 * experts), jnp.bfloat16),
-        ],
-        axis=1,
-    )
-    gate_w = jnp.transpose(gate_up[0], (1, 0, 2)).reshape(2, shares, share, hidden)
-    gate_w = jnp.pad(gate_w, ((0, 0), (0, 0), (0, wide - share), (0, 0)))
-    down_w = jnp.transpose(down_weight[0].reshape(hidden, shares, share), (1, 0, 2))
-    stream_share = lax.dynamic_slice_in_dim(stream, column_start, share, 1)
-    mixture = moe((experts // cores, cores, shares, pairs, share), own_rows, gate_w, down_w)
-    return (stream_share + mixture).astype(jnp.bfloat16)
+    weights = jnp.concatenate([high, dense - high], axis=1).astype(jnp.bfloat16)
+    tail = jnp.pad(weights, ((0, 0), (share, wide - share - 2 * experts)))
+    spare = (0, wide - share)
+    parts = jnp.transpose(
+        partial_value.astype(jnp.bfloat16).reshape(tok_rows, shares, share), (1, 0, 2)
+    )
+    parts = jnp.pad(parts, ((0, 0), (0, 0), spare))
+    own_residual = jnp.pad(
+        lax.dynamic_slice_in_dim(residual, column_start, share, 1), ((0, 0), spare)
+    )
+    own_gain = jnp.pad(lax.dynamic_slice_in_dim(norm_gain, column_start, share, 0), spare)
+    return moe(
+        (experts // cores, cores, shares, pairs, share),
+        parts, own_residual, own_gain[None, :], tail, gate_w, down_w,
+    )
 
 
 def solution(mesh):

time: 216 us -> 194 us (0.90)
  waiting for transfers between devices: 25.2 us -> 0.04 us
  Pallas kernels: 102 us -> 117 us
  local copies, waits for them, and re-layouts: 41.7 us -> 33.9 us
  other arithmetic: 12.7 us -> 9.44 us
    all_gather x1, waiting for transfers between devices: 25.1 us -> 0.02 us  [per_device(): key_piece = lax.all_gather(keys_values, 'tok', axis=0, tiled=True)]
    pallas_call x1, Pallas kernels: 102 us -> 117 us  [moe(): pl.pallas_call(functools.partial(moe_kernel, dims), out_shape=jax.ShapeDt...]
    pad x1 -> x4, local copies, waits for them, and re-layouts: 8.02 us -> 2.58 us  [the longest x1 0.95 us: per_device(): parts = jnp.pad(parts, ((0, 0), (0, 0), spare))]
    convert_element_type x3 -> x0, local copies, waits for them, and re-layouts: 2.21 us -> none  [the longest x1 1.17 us: per_device(): partial_value.astype(jnp.bfloat16)]
    unnamed x20 -> x26, local copies, waits for them, and re-layouts: 11 us -> 9.74 us
  transfers between devices with their start and end apart: 2 -> 1, of which waited for: 1 -> 0; matrix products, arithmetic and copies ran while one was open for 17% -> 15% of each run, Pallas kernels for 0% -> 0%
where the time goes in v2:
time: 194 us; the launch traced here: 193 us
  Pallas kernels  117 us (60%)
  local copies, waits for them, and re-layouts  33.9 us (17%)
  matrix products  19.5 us (10%)
  between operations  13.6 us (7%)
  other arithmetic  9.44 us (5%)
    pallas_call x1, Pallas kernels, moe(): pl.pallas_call(functools.partial(moe_kernel, dims), out_shape=jax.ShapeDt...  117 us
    transpose x1, local copies, waits for them, and re-layouts, per_device(): jnp.transpose(gate_up[0], (1, 0, 2)).reshape(2, shares, share, hidden)  12 us
    unnamed x26, local copies, waits for them, and re-layouts  9.74 us
    reduce_sum x1, other arithmetic, per_device(): totals = totals * decay + jnp.sum(weights, axis=-1)  9.17 us
    dot_general x1, matrix products, per_device(): jnp.einsum('tgrd,ngd->grtn', grouped, split_piece[:, :, 0], preferred_ele...  8.16 us
    dot_general x1, matrix products, per_device(): jnp.einsum('grtn,ngd->grtd', weights.astype(jnp.bfloat16), split_piece[:,...  8.13 us
    another operation x1, local copies, waits for them, and re-layouts, per_device(): down_weight[0].reshape(hidden, shares, share)  6.54 us
  transfers between devices with their start and end apart: 1, of which 0 were waited for; matrix products, arithmetic and copies ran while one was open for 15% of the time, Pallas kernels for 0%

profile of v2, /device:TPU:0, one launch (start us, length us, event | category | flops | bytes accessed | tf_op | source)
XLA Modules:
  0.0 193.2 jit_solution(7058467046188529321)
XLA Ops:
  6.5 0.0 copy-start
  6.5 0.0 all-gather.2.cloned.1.call-start
  6.5 1.7 copy.45
  8.3 0.0 all-gather.2.cloned.1.call-update
  8.3 0.0 copy-start.2
  8.3 0.0 copy-start.7
  8.3 0.0 copy-start.4
  8.3 0.0 copy-start.5
  8.4 0.0 copy-start.6
  8.4 12.0 %copy.46 = bf16[2,2880,720]{2,1,0:T(8,128)(2,1)} copy(bf16[2,2880,720]{1,2,0:T(8,128)(2,1)} %bitcast.59) | data formatting | bytes 16588800 | tf_op jit(solution)/shard_map/transpose | solution.py:434
  20.3 6.5 %copy.47 = bf16[1,720,2880]{1,2,0:T(8,128)(2,1)} copy(bf16[1,720,2880]{2,1,0:T(8,128)(2,1)} %param.19) | data formatting | bytes 8294400 | tf_op args[9]
  26.9 6.5 %copy.48 = bf16[720,2,1440]{2,0,1:T(8,128)(2,1)} copy(bf16[720,2,1440]{0,2,1:T(8,128)(2,1)} %bitcast.57) | data formatting | bytes 8294400 | tf_op jit(solution)/shard_map/reshape;squeeze | solution.py:435
  33.4 0.0 copy-done.2
  33.4 0.3 copy.50
  33.7 0.0 copy-done.7
  33.7 0.1 broadcast_in_dim.41
  33.8 0.0 copy-done
  33.8 0.2 copy.62
  34.0 0.0 copy-done.4
  34.0 0.1 dynamic_slice.7
  34.1 0.6 broadcast_in_dim.46.gain_ref
  34.7 0.0 copy-done.5
  34.7 0.0 copy-done.6
  34.7 0.1 copy.55
  34.9 0.8 pad.17.residual_ref
  35.6 0.8 pad.19.tail_ref
  36.5 0.1 iota_compare_fusion
  36.6 0.0 all-gather.2.cloned.1.call-done
  36.6 0.0 copy-start.3
  36.6 8.2 %fusion.2 = (f32[4,8,128]{2,1,0:T(8,128)S(1)}, f32[4,1024,128,8]{2,1,3,0:T(8,128)}) fusion(pred[128,1024]{0,1:T(8,128)(4,1)S(1)} %iota_compare_fusion, bf16[128,4,8,64]{0,3,2,1:T(8,128)(2,1)S(1)} %bitcast.62, bf16[1024,4,2,64]{0,3,2,1:T(8,128)(2,1)} %bitcast.64), kind=kOutput, calls=%fused_computation.4 | convolution fusion | flops 549449728 | bytes 17973248 | tf_op jit(solution)/shard_map/tgrd,ngd->grtn/dot_general | solution.py:442
  44.8 0.1 broadcast_maximum_fusion
  44.9 9.2 %fusion = f32[4,8,128]{2,1,0:T(8,128)S(1)} fusion(f32[4,1024,128,8]{2,1,3,0:T(8,128)} %get-tuple-element.16, f32[4,8,128]{2,1,0:T(8,128)S(1)} %broadcast_maximum_fusion, pred[128,1024]{0,1:T(8,128)(4,1)S(1)} %iota_compare_fusion), kind=kLoop, calls=%fused_computation.2 | loop fusion | flops 16773120 | bytes 16941056 | tf_op jit(solution)/shard_map/reduce_sum | solution.py:453
  54.0 0.0 slice-start
  54.0 0.1 multiply_bitcast_fusion
  54.1 0.0 copy-done.3
  54.1 0.0 slice-start.1
  54.1 0.0 slice-start.2
  54.2 8.1 %divide_convert_fusion = bf16[128,4,8,64]{0,3,2,1:T(8,128)(2,1)S(1)} fusion(f32[4,1024,128,8]{2,1,3,0:T(8,128)} %get-tuple-element.16, f32[4,8,128]{2,1,0:T(8,128)S(1)} %broadcast_maximum_fusion, pred[128,1024]{0,1:T(8,128)(4,1)S(1)} %iota_compare_fusion, bf16[1024,4,2,64]{0,3,2,1:T(8,128)(2,1)S(1)} %bitcast.65, f32[128,4,8]{0,2,1:T(8,128)S(1)} %get-tuple-element.12, ...), kind=kOutput, calls=%fused_computation.10 | convolution fusion | flops 554434560 | bytes 18006016 | tf_op jit(solution)/shard_map/grtn,ngd->grtd/dot_general | solution.py:454
  62.3 0.0 slice-done
  62.3 0.0 slice-done.1
  62.3 1.0 slice-done.2
  63.3 3.2 %convolution_convert_fusion = bf16[128,2880]{0,1:T(8,128)(2,1)S(1)} fusion(bf16[2048,2880]{0,1:T(8,128)(2,1)S(1)} %bitcast.67, bf16[128,2048]{0,1:T(8,128)(2,1)S(1)} %bitcast.68), kind=kOutput, calls=%fused_computation.7 | convolution fusion | flops 1510318080 | bytes 13058048 | tf_op jit(solution)/shard_map/dot_general | solution.py:467
  66.5 0.3 copy.53
  66.8 0.0 copy-start.1
  66.8 1.0 pad.16.parts_ref
  67.8 116.7 %shard_map.100 = bf16[128,1440]{1,0:T(8,128)(2,1)} custom-call(bf16[2,128,1536]{2,1,0:T(8,128)(2,1)} %pad.16.parts_ref, bf16[128,1536]{1,0:T(8,128)(2,1)} %pad.17.residual_ref, f32[1,1536]{1,0:T(1,128)} %broadcast_in_dim.46.gain_ref, bf16[128,1536]{1,0:T(8,128)(2,1)} %pad.19.tail_ref, bf16[2,2,1440,720]{3,2,1,0:T(8,128)(2,1)} %bitcast.58, ...), custom_call_target="tpu_custom_call" | custom-call | flops 12740198400 | bytes 12441600 | tf_op jit(solution)/shard_map/pallas_call | solution.py:353
  184.4 1.9 copy.56
  186.4 0.0 copy-done.1
  (7 shorter events, 0.1 us)
Async XLA Ops:
  6.5 27.2 %copy-start = (bf16[128,2880]{0,1:T(8,128)(2,1)S(1)}, bf16[128,2880]{0,1:T(8,128)(2,1)}, u32[]{:S(2)}) copy-start(bf16[128,2880]{0,1:T(8,128)(2,1)} %param.13) | copy-start | bytes 2211844
  6.5 30.1 %all-gather.2.cloned.1.call-start = ((), (), s32[]{:S(2)}) async-start(), calls=%async_computation | async-start | bytes 1179648 | tf_op jit(solution)/shard_map/all_gather | solution.py:430
  8.3 25.1 %copy-start.2 = (bf16[128,2048]{1,0:T(8,128)(2,1)S(1)}, bf16[128,2048]{1,0:T(8,128)(2,1)}, u32[]{:S(2)}) copy-start(bf16[128,2048]{1,0:T(8,128)(2,1)} %param.10) | copy-start | bytes 1572868
  8.3 25.4 %copy-start.7 = (f32[32]{0:T(128)S(1)}, f32[32]{0:T(128)}, u32[]{:S(2)}) copy-start(f32[32]{0:T(128)} %param.12) | copy-start | bytes 388
  8.3 25.7 %copy-start.4 = (f32[2880]{0:T(1024)S(1)}, f32[2880]{0:T(1024)}, u32[]{:S(2)}) copy-start(f32[2880]{0:T(1024)} %param.15) | copy-start | bytes 34564
  8.3 26.4 %copy-start.5 = (f32[128,4]{0,1:T(4,128)S(1)}, f32[128,4]{0,1:T(4,128)}, u32[]{:S(2)}) copy-start(f32[128,4]{0,1:T(4,128)} %param.17) | copy-start | bytes 6148
  8.4 26.4 %copy-start.6 = (s32[128,4]{0,1:T(4,128)S(1)}, s32[128,4]{0,1:T(4,128)}, u32[]{:S(2)}) copy-start(s32[128,4]{0,1:T(4,128)} %param.16) | copy-start | bytes 6148
  36.6 17.5 %copy-start.3 = (bf16[1024,512]{0,1:T(8,128)(2,1)S(1)}, bf16[1024,512]{0,1:T(8,128)(2,1)}, u32[]{:S(2)}) copy-start(bf16[1024,512]{0,1:T(8,128)(2,1)} %all-gather.2.cloned.1.call-done) | copy-start | bytes 3145732
  54.0 8.3 %slice-start = ((s8[11796480]{0:T(1024)(128)(4,1)}), s8[4194304]{0:T(1024)(128)(4,1)S(1)}, s32[]{:S(2)}) async-start(s8[11796480]{0:T(1024)(128)(4,1)} %bitcast.66), calls=%async_computation.1 | async-start | bytes 8388608
  54.1 8.2 %slice-start.1 = ((s8[11796480]{0:T(1024)(128)(4,1)}), s8[4194304]{0:T(1024)(128)(4,1)S(1)}, s32[]{:S(2)}) async-start(s8[11796480]{0:T(1024)(128)(4,1)} %bitcast.66), calls=%async_computation.2 | async-start | bytes 8388608
  54.1 9.1 %slice-start.2 = ((s8[11796480]{0:T(1024)(128)(4,1)}), s8[3407872]{0:T(1024)(128)(4,1)S(1)}, s32[]{:S(2)}) async-start(s8[11796480]{0:T(1024)(128)(4,1)} %bitcast.66), calls=%async_computation.3 | async-start | bytes 6815744
  66.8 119.6 %copy-start.1 = (bf16[128,2880]{0,1:T(8,128)(2,1)S(1)}, bf16[128,2880]{0,1:T(8,128)(2,1)}, u32[]{:S(2)}) copy-start(bf16[128,2880]{0,1:T(8,128)(2,1)} %param.13) | copy-start | bytes 2211844
Sparse Core Ops, SparseCore 0:
  8.9 26.5 all-gather.1
